TPU v7x, 16 devices: a whole 2x2x2 slice. The times are simulated.
16 devices in a mesh: dp: 1, tp: 16 (over x, y, z, core).
Axes of the slice: x: 2, y: 2, z: 2, core: 2. Of those that a mesh axis runs over, the one named last changes fastest.
Arguments:
- x: bfloat16 [2048, 8192], P('dp')
- w_gate: bfloat16 [8192, 32768], P(None, 'tp')
- w_up: bfloat16 [8192, 32768], P(None, 'tp')
- w_down: bfloat16 [32768, 8192], P('tp')
Outputs:
- output: bfloat16 [2048, 8192], P('dp')
All inputs are finite; a program needn't handle non-finite values.
Results may differ from a plain program's by a relative error of at most 0.016.
Values are sent between devices in bfloat16 or wider.
A program may use at most 2 GiB of HBM per device.

v0:
```python
import jax
import jax.numpy as jnp
from jax import lax
from jax.sharding import PartitionSpec as P


def solution(mesh):
    def step(x, w_gate, w_up, w_down):
        gate = jnp.dot(x, w_gate, preferred_element_type=jnp.float32)
        up = jnp.dot(x, w_up, preferred_element_type=jnp.float32)
        hidden = (jax.nn.silu(gate) * up).astype(jnp.bfloat16)
        term = jnp.dot(hidden, w_down, preferred_element_type=jnp.float32).astype(jnp.bfloat16)
        return lax.psum(term, "tp")

    return jax.shard_map(
        step,
        mesh=mesh,
        in_specs=(P("dp", None), P(None, "tp"), P(None, "tp"), P("tp", None)),
        out_specs=P("dp", None),
        check_vma=False,
    )
```

profile of v0, /device:TPU:0, one launch (start us, length us, event | category | flops | bytes accessed | tf_op | source)
XLA Modules:
  0.0 596.4 jit_solution(3639848689786766745)
XLA Ops:
  6.5 0.0 all-reduce.2.cloned.1.call-start
  6.5 79.3 %fusion = f32[2048,2048]{1,0:T(8,128)} fusion(bf16[2048,8192]{1,0:T(8,128)(2,1)} %param.4, bf16[8192,2048]{1,0:T(8,128)(2,1)} %param.5), kind=kOutput, calls=%fused_computation.2 | convolution fusion | flops 68719476736 | bytes 83886080 | tf_op jit(solution)/shard_map/dot_general | solution.py:9
  85.8 83.1 %multiply_convert_fusion = bf16[2048,2048]{1,0:T(8,128)(2,1)} fusion(f32[2048,2048]{1,0:T(8,128)} %fusion, bf16[2048,8192]{1,0:T(8,128)(2,1)} %param.4, bf16[8192,2048]{1,0:T(8,128)(2,1)} %param.6), kind=kOutput, calls=%fused_computation.1 | convolution fusion | flops 68744642560 | bytes 92274688 | tf_op jit(solution)/shard_map/dot_general | solution.py:10
  168.9 77.9 %convolution_convert_fusion = bf16[2048,8192]{1,0:T(8,128)(2,1)} fusion(bf16[2048,2048]{1,0:T(8,128)(2,1)} %multiply_convert_fusion, bf16[2048,8192]{1,0:T(8,128)(2,1)} %param.7), kind=kOutput, calls=%fused_computation | convolution fusion | flops 68736253952 | bytes 75497472 | tf_op jit(solution)/shard_map/dot_general | solution.py:12
  246.8 0.0 all-reduce.2.cloned.1.call-update
  246.9 319.7 %all-reduce.2.cloned.1.call-done = bf16[2048,8192]{1,0:T(8,128)(2,1)} async-done(((bf16[2048,8192]{1,0:T(8,128)(2,1)}), bf16[2048,8192]{1,0:T(8,128)(2,1)}) %all-reduce.2.cloned.1.call-update) | async-done | bytes 33554448 | tf_op jit(solution)/shard_map/psum | solution.py:13
  566.5 23.0 %copy.6 = bf16[2048,8192]{1,0:T(8,128)(2,1)} copy(bf16[2048,8192]{1,0:T(8,128)(2,1)} %all-reduce.2.cloned.1.call-done) | data formatting | bytes 67108864
Async XLA Ops:
  6.5 560.0 %all-reduce.2.cloned.1.call-start = ((), (), s32[]{:S(2)}) async-start(), calls=%async_computation | async-start | bytes 67108864 | tf_op jit(solution)/shard_map/psum | solution.py:13
Sparse Core Ops, SparseCore 0:
  247.0 319.5 all-reduce.1
where the time goes:
time: 596 us
  waiting for transfers between devices  320 us (54%)
  matrix products  240 us (40%)
  local copies, waits for them, and re-layouts  23 us (4%)
  between operations  13.4 us (2%)
    psum x1, waiting for transfers between devices, step(): return lax.psum(term, 'tp')  320 us
    dot_general x1, matrix products, step(): up = jnp.dot(x, w_up, preferred_element_type=jnp.float32)  83.1 us
    dot_general x1, matrix products, step(): gate = jnp.dot(x, w_gate, preferred_element_type=jnp.float32)  79.3 us
    dot_general x1, matrix products, step(): jnp.dot(hidden, w_down, preferred_element_type=jnp.float32)  77.9 us
    unnamed x1, local copies, waits for them, and re-layouts  23 us
  transfers between devices with their start and end apart: 1, of which 1 were waited for; matrix products, arithmetic and copies ran while one was open for 0% of the time, Pallas kernels for 0%

commit v1 on v0

v1 whole, which is shorter than its diff:
```python
import functools

import jax
import jax.numpy as jnp
from jax import lax
from jax.experimental import pallas as pl
from jax.experimental.pallas import tpu as pltpu
from jax.sharding import PartitionSpec as P

MESH = pl.DeviceIdType.MESH
CHUNK = 512
TILES = 8
SLOTS = 8
KEEP = 3

EVENTS = (
    ("gather_core_wait", 7, 0),
    ("gather_core", 6, 1),
    ("gather3", 5, 0),
    ("gather2", 4, 0),
    ("gather1", 3, 1),
    ("sum3", 2, 2),
    ("sum2", 1, 2),
)


def kernel(
    x_ref, gate_ref, up_ref, down_ref, y_ref, other_ref,
    xb, gb, ub, db, hidden, gated,
    part, send1, keep2, send2, keep3, send3, final, recv1, recv2, recv3,
    load_sem, x_sem, down_sem, hid_send, hid_recv, other_send, other_recv, local_sem, send_sem, recv_sem,
):
    rows, depth = x_ref.shape
    width = gate_ref.shape[1]
    half = depth // 2
    tile, group = width // TILES, half // TILES
    chunks = rows // CHUNK
    n = chunks * TILES
    me = lax.axis_index("tp")
    core = lax.rem(me, 2)
    partner = me + 1 - 2 * core

    def to(device):
        return {"tp": device}

    def remote(src, dst, send, recv, device):
        return pltpu.make_async_remote_copy(
            src_ref=src, dst_ref=dst, send_sem=send, recv_sem=recv, device_id=to(device), device_id_type=MESH
        )

    def axis(d):
        d = lax.rem(d, 3)
        mask = 2 + d + d * d
        bit = lax.rem(me // mask, 2)
        return bit, me + mask * (1 - 2 * bit)

    barrier = pltpu.get_barrier_semaphore()
    for device in (partner, axis(0)[1], axis(1)[1], axis(2)[1]):
        pl.semaphore_signal(barrier, inc=1, device_id=to(device), device_id_type=MESH)
    pl.semaphore_wait(barrier, 4)

    def load_x(c):
        slot = lax.rem(c, 2)
        return pltpu.make_async_copy(
            x_ref.at[pl.ds(pl.multiple_of(c * CHUNK, CHUNK), CHUNK)], xb.at[slot], x_sem.at[slot]
        )

    def columns(t, size):
        return pl.ds(pl.multiple_of(t * size, size), size)

    def load_gate(i):
        return pltpu.make_async_copy(gate_ref.at[:, columns(lax.rem(i, TILES), tile)], gb, load_sem.at[0])

    def load_up(i):
        return pltpu.make_async_copy(up_ref.at[:, columns(lax.rem(i, TILES), tile)], ub, load_sem.at[1])

    def load_down(g):
        j = lax.rem(g, TILES)
        mine = pl.ds(pl.multiple_of(core * half + j * group, group), group)
        return (
            pltpu.make_async_copy(down_ref.at[:, mine], db.at[pl.ds(0, width)], down_sem.at[0]),
            pltpu.make_async_copy(other_ref.at[:, columns(j, group)], db.at[pl.ds(width, width)], down_sem.at[1]),
        )

    theirs = pl.ds(pl.multiple_of((1 - core) * half, half), half)
    swap_down = remote(down_ref.at[:, theirs], other_ref, other_send, other_recv, partner)

    def swap_hidden(i):
        slot, t = lax.rem(i // TILES, 2), lax.rem(i, TILES)
        return remote(
            hidden.at[slot, :, columns(t, tile)],
            hidden.at[slot, :, pl.ds(pl.multiple_of(width + t * tile, tile), tile)],
            hid_send.at[slot, t], hid_recv.at[slot, t], partner,
        )

    class Group:
        def __init__(self, g):
            self.s, self.k = lax.rem(g, SLOTS), lax.rem(g, KEEP)
            rot = lax.rem(g, 3)
            (self.b1, self.n1), (self.b2, self.n2), (self.b3, self.n3) = axis(rot), axis(rot + 1), axis(rot + 2)
            self.r0 = (g // TILES) * CHUNK
            self.r1 = self.r0 + self.b1 * (CHUNK // 2)
            self.r2 = self.r1 + self.b2 * (CHUNK // 4)
            self.r3 = self.r2 + self.b3 * (CHUNK // 8)
            self.cols = pl.ds(pl.multiple_of(core * half + lax.rem(g, TILES) * group, group), group)

        def copy(self, stage, src, dst, device):
            return remote(src, dst, send_sem.at[stage, self.s], recv_sem.at[stage, self.s], device)

        def reduce1(self):
            return self.copy(0, send1.at[self.k], recv1.at[self.s], self.n1)

        def reduce2(self):
            return self.copy(1, send2.at[self.k], recv2.at[self.s], self.n2)

        def reduce3(self):
            return self.copy(2, send3.at[self.k], recv3.at[self.s], self.n3)

        def window(self, row, size):
            return y_ref.at[pl.ds(pl.multiple_of(row, size), size), self.cols]

        def local(self):
            return pltpu.make_async_copy(
                final.at[self.k], self.window(self.r3, CHUNK // 8), local_sem.at[self.s]
            )

        def gather1(self):
            return self.copy(3, final.at[self.k], self.window(self.r3, CHUNK // 8), self.n3)

        def gather2(self):
            w = self.window(self.r2, CHUNK // 4)
            return self.copy(4, w, w, self.n2)

        def gather3(self):
            w = self.window(self.r1, CHUNK // 2)
            return self.copy(5, w, w, self.n1)

        def gather_core(self):
            w = self.window(self.r0, CHUNK)
            return self.copy(6, w, w, partner)

    def rows_at(bit, size):
        return pl.ds(pl.multiple_of(bit * size, size), size)

    def sum1(g):
        q = Group(g)
        send1[q.k] = part[q.k, rows_at(1 - q.b1, CHUNK // 2)].astype(jnp.bfloat16)
        q.reduce1().start()

    def sum2(g):
        q = Group(g)
        size = CHUNK // 4
        q.reduce1().wait()
        for keep in (False, True):
            bit = q.b2 if keep else 1 - q.b2
            mine = part[q.k, pl.ds(pl.multiple_of(q.b1 * (CHUNK // 2) + bit * size, size), size)]
            total = mine + recv1[q.s, rows_at(bit, size)].astype(jnp.float32)
            if keep:
                keep2[q.k] = total
            else:
                send2[q.k] = total.astype(jnp.bfloat16)
                q.reduce2().start()

    def sum3(g):
        q = Group(g)
        size = CHUNK // 8
        q.reduce2().wait()
        for keep in (False, True):
            bit = q.b3 if keep else 1 - q.b3
            total = keep2[q.k, rows_at(bit, size)] + recv2[q.s, rows_at(bit, size)].astype(jnp.float32)
            if keep:
                keep3[q.k] = total
            else:
                send3[q.k] = total.astype(jnp.bfloat16)
                q.reduce3().start()

    def gather1(g):
        q = Group(g)
        q.reduce3().wait()
        final[q.k] = (keep3[q.k] + recv3[q.s].astype(jnp.float32)).astype(jnp.bfloat16)
        q.gather1().start()
        q.local().start()

    def gather2(g):
        q = Group(g)
        q.gather1().wait()
        q.local().wait()
        q.gather2().start()

    def gather3(g):
        q = Group(g)
        q.gather2().wait()
        q.gather3().start()

    def gather_core(g):
        q = Group(g)
        q.gather3().wait()
        q.gather_core().start()

    def gather_core_wait(g):
        Group(g).gather_core().wait()

    stages = dict(
        sum2=sum2, sum3=sum3, gather1=gather1, gather2=gather2, gather3=gather3,
        gather_core=gather_core, gather_core_wait=gather_core_wait,
    )

    def events(i, place):
        for name, delay, where in EVENTS:
            if where == place:
                g = i - TILES - delay
                pl.when((g >= 0) & (g < n))(functools.partial(stages[name], g))

    load_x(0).start()
    load_gate(0).start()
    load_up(0).start()

    def body(i, carry):
        slot, t = lax.rem(i // TILES, 2), lax.rem(i, TILES)
        g = i - TILES

        @pl.when(i < n)
        def _():
            pl.when(t == 0)(lambda: load_x(i // TILES).wait())
            load_gate(i).wait()
            gated[...] = jnp.dot(xb[slot], gb[...], preferred_element_type=jnp.float32)
            pl.when(i + 1 < n)(lambda: load_gate(i + 1).start())

        @pl.when(i == 0)
        def _():
            swap_down.start()
            if chunks > 1:
                load_x(1).start()

        events(i, 0)

        @pl.when((g >= 0) & (g < n))
        def _():
            @pl.when(lax.rem(g, TILES) == 0)
            def _():
                for t in range(TILES):
                    swap_hidden((g // TILES) * TILES + t).wait()

            for copy in load_down(g):
                copy.wait()
            part[lax.rem(g, KEEP)] = jnp.dot(
                hidden[lax.rem(g // TILES, 2)], db[...], preferred_element_type=jnp.float32
            )
            sum1(g)

        @pl.when(g == -1)
        def _():
            swap_down.wait()

        @pl.when((g >= -1) & (g < n - 1))
        def _():
            for copy in load_down(g + 1):
                copy.start()

        events(i, 1)

        @pl.when(i < n)
        def _():
            load_up(i).wait()
            up = jnp.dot(xb[slot], ub[...], preferred_element_type=jnp.float32)
            pl.when(i + 1 < n)(lambda: load_up(i + 1).start())
            hidden[slot, :, columns(t, tile)] = (jax.nn.silu(gated[...]) * up).astype(jnp.bfloat16)
            swap_hidden(i).start()
            pl.when((t == TILES - 1) & (i // TILES + 2 < chunks))(lambda: load_x(i // TILES + 2).start())

        events(i, 2)
        return carry

    lax.fori_loop(0, n + TILES + 1 + max(e[1] for e in EVENTS), body, 0)


def block(x, w_gate, w_up, w_down):
    rows, depth = x.shape
    width = w_gate.shape[1]
    half = depth // 2
    tile, group = width // TILES, half // TILES
    b16, f32 = jnp.bfloat16, jnp.float32
    dma = pltpu.SemaphoreType.DMA
    flops = 6 * rows * depth * width
    y, _ = pl.pallas_call(
        kernel,
        out_shape=(jax.ShapeDtypeStruct((rows, depth), b16), jax.ShapeDtypeStruct((width, half), b16)),
        in_specs=[pl.BlockSpec(memory_space=pl.ANY)] * 4,
        out_specs=(pl.BlockSpec(memory_space=pl.ANY),) * 2,
        scratch_shapes=[
            pltpu.VMEM((2, CHUNK, depth), b16),
            pltpu.VMEM((depth, tile), b16),
            pltpu.VMEM((depth, tile), b16),
            pltpu.VMEM((2 * width, group), b16),
            pltpu.VMEM((2, CHUNK, 2 * width), b16),
            pltpu.VMEM((CHUNK, tile), f32),
            pltpu.VMEM((KEEP, CHUNK, group), f32),
            pltpu.VMEM((KEEP, CHUNK // 2, group), b16),
            pltpu.VMEM((KEEP, CHUNK // 4, group), f32),
            pltpu.VMEM((KEEP, CHUNK // 4, group), b16),
            pltpu.VMEM((KEEP, CHUNK // 8, group), f32),
            pltpu.VMEM((KEEP, CHUNK // 8, group), b16),
            pltpu.VMEM((KEEP, CHUNK // 8, group), b16),
            pltpu.VMEM((SLOTS, CHUNK // 2, group), b16),
            pltpu.VMEM((SLOTS, CHUNK // 4, group), b16),
            pltpu.VMEM((SLOTS, CHUNK // 8, group), b16),
            dma((2,)), dma((2,)), dma((2,)), dma((2, TILES)), dma((2, TILES)), dma, dma, dma((SLOTS,)),
            dma((7, SLOTS)), dma((7, SLOTS)),
        ],
        compiler_params=pltpu.CompilerParams(
            collective_id=0, has_side_effects=True, vmem_limit_bytes=64_000_000
        ),
        cost_estimate=pl.CostEstimate(flops=flops, bytes_accessed=8 * depth * width, transcendentals=rows * width),
    )(x, w_gate, w_up, w_down)
    return y


def solution(mesh):
    return jax.shard_map(
        block,
        mesh=mesh,
        in_specs=(P("dp", None), P(None, "tp"), P(None, "tp"), P("tp", None)),
        out_specs=P("dp", None),
        check_vma=False,
    )
```

time: 596 us -> 370 us (0.62)
  Pallas kernels: 0 us -> 347 us
  waiting for transfers between devices: 320 us -> 0 us
  matrix products: 240 us -> 0 us
  between operations: 13.4 us -> 0.01 us
    pallas_call x0 -> x1, Pallas kernels: none -> 347 us  [block(): pl.pallas_call(kernel, out_shape=(jax.ShapeDtypeStruct((rows, depth), b16...]
    psum x1 -> x0, waiting for transfers between devices: 320 us -> none  [step(): return lax.psum(term, 'tp')]
    dot_general x3 -> x0, matrix products: 240 us -> none  [the longest x1 83.1 us: step(): up = jnp.dot(x, w_up, preferred_element_type=jnp.float32)]
  transfers between devices with their start and end apart: 1 -> 0, of which waited for: 1 -> 0; matrix products, arithmetic and copies ran while one was open for 0% -> 0% of each run, Pallas kernels for 0% -> 0%
where the time goes in v1:
time: 370 us
  Pallas kernels  347 us (94%)
  local copies, waits for them, and re-layouts  23 us (6%)
    pallas_call x1, Pallas kernels, block(): pl.pallas_call(kernel, out_shape=(jax.ShapeDtypeStruct((rows, depth), b16...  347 us
    unnamed x1, local copies, waits for them, and re-layouts  23 us

profile of v1, /device:TPU:0, one launch (start us, length us, event | category | flops | bytes accessed | tf_op | source)
XLA Modules:
  0.0 369.9 jit_solution(10178012765305756771)
XLA Ops:
  0.0 346.9 %shard_map.46 = (bf16[2048,8192]{1,0:T(8,128)(2,1)}, bf16[2048,4096]{1,0:T(8,128)(2,1)}) custom-call(bf16[2048,8192]{1,0:T(8,128)(2,1)} %x_ref.1, bf16[8192,2048]{1,0:T(8,128)(2,1)} %gate_ref.1, bf16[8192,2048]{1,0:T(8,128)(2,1)} %up_ref.1, bf16[2048,8192]{1,0:T(8,128)(2,1)} %down_ref.1), custom_call_target="tpu_custom_call" | custom-call | flops 206158430208 | bytes 134217728 | tf_op jit(solution)/shard_map/pallas_call | solution.py:285
  346.9 23.0 %copy.6 = bf16[2048,8192]{1,0:T(8,128)(2,1)} copy(bf16[2048,8192]{1,0:T(8,128)(2,1)} %get-tuple-element.6) | data formatting | bytes 67108864

commit v2 on v0

v2 whole, which is shorter than its diff:
```python
import functools

import jax
import jax.numpy as jnp
from jax import lax
from jax.experimental import pallas as pl
from jax.experimental.pallas import tpu as pltpu
from jax.sharding import PartitionSpec as P

MESH = pl.DeviceIdType.MESH
SIZES = (512, 384, 384, 384, 384)
TILES = 8
SLOTS = 12
KEEP = 3
PARTS = ((0, 4),)
TURN = 1
SPLIT = 4

EVENTS = (
    ("gather_core_wait", 27, 0, 0, 22),
    ("gather_core", 11, 0, 0, 22),
    ("gather_core", 23, 0, 29, 40),
    ("gather3", 14, 0, 29, 40),
    ("gather2", 6, 0, 22, 29),
    ("gather1", 5, 0, 0, 29),
    ("gather1", 8, 0, 29, 40),
    ("sum3", 4, 0, 0, 22),
    ("sum3", 5, 0, 29, 40),
    ("sum2", 2, 0, 22, 29),
    ("gather_core_wait", 26, 1, 22, 29),
    ("gather_core_wait", 28, 1, 29, 40),
    ("gather_core", 11, 1, 22, 29),
    ("gather3", 8, 1, 0, 29),
    ("gather2", 6, 1, 0, 22),
    ("gather2", 10, 1, 29, 40),
    ("sum3", 3, 1, 22, 29),
    ("sum2", 2, 1, 0, 22),
    ("sum2", 2, 1, 29, 40),
)


def phases():
    runs, row = [], 0
    for c, size in enumerate(SIZES):
        if runs and runs[-1][2] == size:
            runs[-1][1] = c + 1
        else:
            runs.append([c, c + 1, size, row])
        row += size
    return runs


def kernel(
    x_ref, gate_ref, up_ref, down_ref, y_ref, other_ref,
    xb, gb, ub, db, hidden, gated,
    part, send1, keep2, send2, keep3, send3, final, recv1, recv2, recv3,
    load_sem, first_sem, x_sem, down_sem, hid_send, hid_recv, other_send, other_recv, local_sem, send_sem, recv_sem,
    core_send, core_recv,
):
    rows, depth = x_ref.shape
    width = gate_ref.shape[1]
    half = depth // 2
    tile, group = width // TILES, half // TILES
    chunks = len(SIZES)
    n = chunks * TILES
    parts = tuple((a * group // 4, b * group // 4) for a, b in PARTS)
    me = lax.axis_index("tp")
    core = lax.rem(me, 2)
    partner = me + 1 - 2 * core

    def to(device):
        return {"tp": device}

    def remote(src, dst, send, recv, device):
        return pltpu.make_async_remote_copy(
            src_ref=src, dst_ref=dst, send_sem=send, recv_sem=recv, device_id=to(device), device_id_type=MESH
        )

    def axis(d):
        d = lax.rem(d, 3)
        mask = 2 + d + d * d
        bit = lax.rem(me // mask, 2)
        return bit, me + mask * (1 - 2 * bit)

    barrier = pltpu.get_barrier_semaphore()
    for device in (partner, axis(0)[1], axis(1)[1], axis(2)[1]):
        pl.semaphore_signal(barrier, inc=1, device_id=to(device), device_id_type=MESH)
    pl.semaphore_wait(barrier, 4)

    def by_size(c, do):
        for first, last, size, row in phases():
            pl.when((c >= first) & (c < last))(functools.partial(do, size, row + (c - first) * size))

    def load_x(c):
        slot = lax.rem(c, 2)

        def copy(size, row):
            rows_ = pl.ds(pl.multiple_of(row, 128), size)
            return pltpu.make_async_copy(x_ref.at[rows_], xb.at[slot, pl.ds(0, size)], x_sem.at[slot])

        return copy

    def start_x(c):
        by_size(c, lambda size, row: load_x(c)(size, row).start())

    def first_loads():
        step = depth // SPLIT
        for k in range(SPLIT):
            cut = pl.ds(k * step, step)
            yield (
                pltpu.make_async_copy(
                    x_ref.at[pl.ds(0, SIZES[0]), cut], xb.at[0, pl.ds(0, SIZES[0]), cut], first_sem.at[0, k]
                ),
                pltpu.make_async_copy(gate_ref.at[cut, pl.ds(0, tile)], gb.at[0, cut], first_sem.at[1, k]),
            )

    def columns(t, size):
        return pl.ds(pl.multiple_of(t * size, size), size)

    def load_gate(i):
        return pltpu.make_async_copy(gate_ref.at[:, columns(lax.rem(i, TILES), tile)], gb.at[lax.rem(i, 2)], load_sem.at[0, lax.rem(i, 2)])

    def load_up(i):
        return pltpu.make_async_copy(up_ref.at[:, columns(lax.rem(i, TILES), tile)], ub.at[lax.rem(i, 2)], load_sem.at[1, lax.rem(i, 2)])

    def load_down(g):
        j = lax.rem(g, TILES)
        mine = pl.ds(pl.multiple_of(core * half + j * group, group), group)
        return (
            pltpu.make_async_copy(down_ref.at[:, mine], db.at[pl.ds(0, width)], down_sem.at[0]),
            pltpu.make_async_copy(other_ref.at[:, columns(j, group)], db.at[pl.ds(width, width)], down_sem.at[1]),
        )

    theirs = pl.ds(pl.multiple_of((1 - core) * half, half), half)
    swap_down = remote(down_ref.at[:, theirs], other_ref, other_send, other_recv, partner)

    def swap_hidden(i, size):
        slot, t = lax.rem(i // TILES, 2), lax.rem(i, TILES)
        return remote(
            hidden.at[slot, pl.ds(0, size), columns(t, tile)],
            hidden.at[slot, pl.ds(0, size), pl.ds(pl.multiple_of(width + t * tile, tile), tile)],
            hid_send.at[slot, t], hid_recv.at[slot, t], partner,
        )

    class Part:
        def __init__(self, g, size, row, p):
            self.p, self.size = p, size
            self.s, self.k = lax.rem(g, SLOTS), lax.rem(g, KEEP)
            (self.b1, self.n1), (self.b2, self.n2), (self.b3, self.n3) = (axis(TURN * g + p + d) for d in range(3))
            self.r1 = row + self.b1 * (size // 2)
            self.r2 = self.r1 + self.b2 * (size // 4)
            self.r3 = self.r2 + self.b3 * (size // 8)
            start, wide = parts[p]
            self.cut = pl.ds(start, wide)
            self.cols = pl.ds(pl.multiple_of(core * half + lax.rem(g, TILES) * group + start, 128), wide)

        def copy(self, stage, src, dst, device):
            return remote(src, dst, send_sem.at[stage, self.p, self.s], recv_sem.at[stage, self.p, self.s], device)

        def reduce(self, stage):
            rows_ = pl.ds(0, self.size >> stage)
            send = (send1, send2, send3)[stage - 1].at[self.k, rows_, self.cut]
            recv = (recv1, recv2, recv3)[stage - 1].at[self.s, rows_, self.cut]
            return self.copy(stage - 1, send, recv, (self.n1, self.n2, self.n3)[stage - 1])

        def window(self, row, size):
            return y_ref.at[pl.ds(pl.multiple_of(row, 16), size), self.cols]

        def final(self):
            return final.at[self.k, pl.ds(0, self.size // 8), self.cut]

        def local(self):
            return pltpu.make_async_copy(
                self.final(), self.window(self.r3, self.size // 8), local_sem.at[self.p, self.s]
            )

        def gather(self, stage):
            if stage == 1:
                return self.copy(3, self.final(), self.window(self.r3, self.size // 8), self.n3)
            if stage == 2:
                w, device = self.window(self.r2, self.size // 4), self.n2
            else:
                w, device = self.window(self.r1, self.size // 2), self.n1
            return self.copy(stage + 2, w, w, device)

    def each_part(do):
        def stage(g, size, row):
            for p in range(len(parts)):
                do(Part(g, size, row, p))

        return stage

    def rows_at(offset, size):
        return pl.ds(pl.multiple_of(offset, 16), size)

    @each_part
    def sum1(q):
        h = q.size // 2
        send1[q.k, 0:h, q.cut] = part[q.k, rows_at((1 - q.b1) * h, h), q.cut].astype(jnp.bfloat16)
        q.reduce(1).start()

    @each_part
    def sum2(q):
        h = q.size // 4
        q.reduce(1).wait()
        for keep in (False, True):
            at = (q.b2 if keep else 1 - q.b2) * h
            total = part[q.k, rows_at(q.b1 * (q.size // 2) + at, h), q.cut] + recv1[
                q.s, rows_at(at, h), q.cut
            ].astype(jnp.float32)
            if keep:
                keep2[q.k, 0:h, q.cut] = total
            else:
                send2[q.k, 0:h, q.cut] = total.astype(jnp.bfloat16)
                q.reduce(2).start()

    @each_part
    def sum3(q):
        h = q.size // 8
        q.reduce(2).wait()
        for keep in (False, True):
            at = (q.b3 if keep else 1 - q.b3) * h
            total = keep2[q.k, rows_at(at, h), q.cut] + recv2[q.s, rows_at(at, h), q.cut].astype(jnp.float32)
            if keep:
                keep3[q.k, 0:h, q.cut] = total
            else:
                send3[q.k, 0:h, q.cut] = total.astype(jnp.bfloat16)
                q.reduce(3).start()

    @each_part
    def gather1(q):
        h = q.size // 8
        q.reduce(3).wait()
        total = keep3[q.k, 0:h, q.cut] + recv3[q.s, 0:h, q.cut].astype(jnp.float32)
        final[q.k, 0:h, q.cut] = total.astype(jnp.bfloat16)
        q.gather(1).start()
        q.local().start()

    @each_part
    def gather2(q):
        q.gather(1).wait()
        q.local().wait()
        q.gather(2).start()

    @each_part
    def gather3(q):
        q.gather(2).wait()
        q.gather(3).start()

    @each_part
    def gathered(q):
        q.gather(3).wait()

    def across(g, size, row):
        cols = pl.ds(pl.multiple_of(core * half + lax.rem(g, TILES) * group, group), group)
        w = y_ref.at[pl.ds(pl.multiple_of(row, 16), size), cols]
        return remote(w, w, core_send.at[g], core_recv.at[g], partner)

    def gather_core(g, size, row):
        gathered(g, size, row)
        across(g, size, row).start()

    def gather_core_wait(g, size, row):
        across(g, size, row).wait()

    stages = dict(
        sum2=sum2, sum3=sum3, gather1=gather1, gather2=gather2, gather3=gather3,
        gather_core=gather_core, gather_core_wait=gather_core_wait,
    )

    def events(i, place):
        for name, delay, where, first, last in EVENTS:
            if where == place:
                g = i - TILES - delay
                pl.when((g >= first) & (g < last))(
                    functools.partial(by_size, g // TILES, functools.partial(stages[name], g))
                )

    for pair in first_loads():
        for copy in pair:
            copy.start()
    load_up(0).start()

    def body(i, carry):
        slot, t = lax.rem(i // TILES, 2), lax.rem(i, TILES)
        g = i - TILES

        @pl.when(i + 1 < n)
        def _():
            load_gate(i + 1).start()
            load_up(i + 1).start()

        def activate(size, gate, up):
            hidden[slot, 0:size, columns(t, tile)] = (jax.nn.silu(gate) * up).astype(jnp.bfloat16)

        @pl.when(i == 0)
        def _():
            step, size = depth // SPLIT, SIZES[0]
            for k, pair in enumerate(first_loads()):
                for copy in pair:
                    copy.wait()
                cut = pl.ds(k * step, step)
                term = jnp.dot(xb[0, 0:size, cut], gb[0, cut], preferred_element_type=jnp.float32)
                gated[...] = term if k == 0 else gated[...] + term
            load_up(0).wait()
            activate(size, gated[...], jnp.dot(xb[0, 0:size], ub[0], preferred_element_type=jnp.float32))
            swap_down.start()
            if chunks > 1:
                start_x(1)

        @pl.when((i > 0) & (i < n))
        def _():
            load_gate(i).wait()
            load_up(i).wait()

            def dots(size, row):
                pl.when(t == 0)(lambda: load_x(i // TILES)(size, row).wait())
                gated[0:size] = jnp.dot(xb[slot, 0:size], gb[lax.rem(i, 2)], preferred_element_type=jnp.float32)
                up = jnp.dot(xb[slot, 0:size], ub[lax.rem(i, 2)], preferred_element_type=jnp.float32)
                activate(size, gated[0:size], up)

            by_size(i // TILES, dots)
            pl.when(t == TILES - 1)(lambda: start_x(i // TILES + 2))

        events(i, 0)
        @pl.when((g >= 0) & (g < n))
        def _():
            for copy in load_down(g):
                copy.wait()

            def dot(size, row):
                @pl.when(lax.rem(g, TILES) == 0)
                def _():
                    for t in range(TILES):
                        swap_hidden((g // TILES) * TILES + t, size).wait()

                part[lax.rem(g, KEEP), 0:size] = jnp.dot(
                    hidden[lax.rem(g // TILES, 2), 0:size], db[...], preferred_element_type=jnp.float32
                )
                sum1(g, size, row)

            by_size(g // TILES, dot)

        pl.when(g == -1)(lambda: swap_down.wait())

        @pl.when((g >= -1) & (g < n - 1))
        def _():
            for copy in load_down(g + 1):
                copy.start()

        pl.when(i < n)(lambda: by_size(i // TILES, lambda size, row: swap_hidden(i, size).start()))
        events(i, 1)
        return carry

    lax.fori_loop(0, n + TILES + 1 + max(e[1] for e in EVENTS), body, 0)


def block(x, w_gate, w_up, w_down):
    rows, depth = x.shape
    width = w_gate.shape[1]
    half = depth // 2
    tile, group, most = width // TILES, half // TILES, max(SIZES)
    b16, f32 = jnp.bfloat16, jnp.float32
    dma = pltpu.SemaphoreType.DMA
    flops = 6 * rows * depth * width
    y, _ = pl.pallas_call(
        kernel,
        out_shape=(jax.ShapeDtypeStruct((rows, depth), b16), jax.ShapeDtypeStruct((width, half), b16)),
        in_specs=[pl.BlockSpec(memory_space=pl.ANY)] * 4,
        out_specs=(pl.BlockSpec(memory_space=pl.ANY),) * 2,
        scratch_shapes=[
            pltpu.VMEM((2, most, depth), b16),
            pltpu.VMEM((2, depth, tile), b16),
            pltpu.VMEM((2, depth, tile), b16),
            pltpu.VMEM((2 * width, group), b16),
            pltpu.VMEM((2, most, 2 * width), b16),
            pltpu.VMEM((most, tile), f32),
            pltpu.VMEM((KEEP, most, group), f32),
            pltpu.VMEM((KEEP, most // 2, group), b16),
            pltpu.VMEM((KEEP, most // 4, group), f32),
            pltpu.VMEM((KEEP, most // 4, group), b16),
            pltpu.VMEM((KEEP, most // 8, group), f32),
            pltpu.VMEM((KEEP, most // 8, group), b16),
            pltpu.VMEM((KEEP, most // 8, group), b16),
            pltpu.VMEM((SLOTS, most // 2, group), b16),
            pltpu.VMEM((SLOTS, most // 4, group), b16),
            pltpu.VMEM((SLOTS, most // 8, group), b16),
            dma((2, 2)), dma((2, SPLIT)), dma((2,)), dma((2,)), dma((2, TILES)), dma((2, TILES)), dma, dma, dma((len(PARTS), SLOTS)),
            dma((6, len(PARTS), SLOTS)), dma((6, len(PARTS), SLOTS)), dma((len(SIZES) * TILES,)), dma((len(SIZES) * TILES,)),
        ],
        compiler_params=pltpu.CompilerParams(
            collective_id=0, has_side_effects=True, vmem_limit_bytes=67_000_000
        ),
        cost_estimate=pl.CostEstimate(flops=flops, bytes_accessed=8 * depth * width, transcendentals=rows * width),
    )(x, w_gate, w_up, w_down)
    return y


def solution(mesh):
    return jax.shard_map(
        block,
        mesh=mesh,
        in_specs=(P("dp", None), P(None, "tp"), P(None, "tp"), P("tp", None)),
        out_specs=P("dp", None),
        check_vma=False,
    )
```

time: 596 us -> 338 us (0.57)
  waiting for transfers between devices: 320 us -> 0 us
  Pallas kernels: 0 us -> 315 us
  matrix products: 240 us -> 0 us
  between operations: 13.4 us -> 0.01 us
    psum x1 -> x0, waiting for transfers between devices: 320 us -> none  [step(): return lax.psum(term, 'tp')]
    pallas_call x0 -> x1, Pallas kernels: none -> 315 us  [block(): pl.pallas_call(kernel, out_shape=(jax.ShapeDtypeStruct((rows, depth), b16...]
    dot_general x3 -> x0, matrix products: 240 us -> none  [the longest x1 83.1 us: step(): up = jnp.dot(x, w_up, preferred_element_type=jnp.float32)]
  transfers between devices with their start and end apart: 1 -> 0, of which waited for: 1 -> 0; matrix products, arithmetic and copies ran while one was open for 0% -> 0% of each run, Pallas kernels for 0% -> 0%
where the time goes in v2:
time: 338 us
  Pallas kernels  315 us (93%)
  local copies, waits for them, and re-layouts  23 us (7%)
    pallas_call x1, Pallas kernels, block(): pl.pallas_call(kernel, out_shape=(jax.ShapeDtypeStruct((rows, depth), b16...  315 us
    unnamed x1, local copies, waits for them, and re-layouts  23 us

profile of v2, /device:TPU:0, one launch (start us, length us, event | category | flops | bytes accessed | tf_op | source)
XLA Modules:
  0.0 337.8 jit_solution(16065393983092075680)
XLA Ops:
  0.0 314.8 %shard_map.46 = (bf16[2048,8192]{1,0:T(8,128)(2,1)}, bf16[2048,4096]{1,0:T(8,128)(2,1)}) custom-call(bf16[2048,8192]{1,0:T(8,128)(2,1)} %x_ref.1, bf16[8192,2048]{1,0:T(8,128)(2,1)} %gate_ref.1, bf16[8192,2048]{1,0:T(8,128)(2,1)} %up_ref.1, bf16[2048,8192]{1,0:T(8,128)(2,1)} %down_ref.1), custom_call_target="tpu_custom_call" | custom-call | flops 206158430208 | bytes 134217728 | tf_op jit(solution)/shard_map/pallas_call | solution.py:366
  314.8 23.0 %copy.6 = bf16[2048,8192]{1,0:T(8,128)(2,1)} copy(bf16[2048,8192]{1,0:T(8,128)(2,1)} %get-tuple-element.6) | data formatting | bytes 67108864

commit v3 on v2

--- a/solution.py
+++ b/solution.py
@@ -17,25 +17,19 @@
 SPLIT = 4
 
 EVENTS = (
-    ("gather_core_wait", 27, 0, 0, 22),
-    ("gather_core", 11, 0, 0, 22),
-    ("gather_core", 23, 0, 29, 40),
-    ("gather3", 14, 0, 29, 40),
-    ("gather2", 6, 0, 22, 29),
-    ("gather1", 5, 0, 0, 29),
-    ("gather1", 8, 0, 29, 40),
-    ("sum3", 4, 0, 0, 22),
-    ("sum3", 5, 0, 29, 40),
-    ("sum2", 2, 0, 22, 29),
-    ("gather_core_wait", 26, 1, 22, 29),
-    ("gather_core_wait", 28, 1, 29, 40),
-    ("gather_core", 11, 1, 22, 29),
-    ("gather3", 8, 1, 0, 29),
-    ("gather2", 6, 1, 0, 22),
-    ("gather2", 10, 1, 29, 40),
-    ("sum3", 3, 1, 22, 29),
-    ("sum2", 2, 1, 0, 22),
-    ("sum2", 2, 1, 29, 40),
+    ("gather_core", 17, 0, 32, 40),
+    ("gather3", 8, 0, 0, 32),
+    ("gather1", 5, 0, 0, 40),
+    ("sum3", 4, 0, 0, 2),
+    ("sum2", 2, 0, 2, 40),
+    ("gather_core_wait", 23, 1, 0, 2),
+    ("gather_core_wait", 26, 1, 2, 32),
+    ("gather_core_wait", 25, 1, 32, 40),
+    ("gather_core", 11, 1, 0, 32),
+    ("gather3", 9, 1, 32, 40),
+    ("gather2", 6, 1, 0, 40),
+    ("sum3", 3, 1, 2, 40),
+    ("sum2", 2, 1, 0, 2),
 )
 
 
@@ -124,11 +118,11 @@
         return pltpu.make_async_copy(up_ref.at[:, columns(lax.rem(i, TILES), tile)], ub.at[lax.rem(i, 2)], load_sem.at[1, lax.rem(i, 2)])
 
     def load_down(g):
-        j = lax.rem(g, TILES)
+        j, s = lax.rem(g, TILES), lax.rem(g, 2)
         mine = pl.ds(pl.multiple_of(core * half + j * group, group), group)
         return (
-            pltpu.make_async_copy(down_ref.at[:, mine], db.at[pl.ds(0, width)], down_sem.at[0]),
-            pltpu.make_async_copy(other_ref.at[:, columns(j, group)], db.at[pl.ds(width, width)], down_sem.at[1]),
+            pltpu.make_async_copy(down_ref.at[:, mine], db.at[s, pl.ds(0, width)], down_sem.at[0, s]),
+            pltpu.make_async_copy(other_ref.at[:, columns(j, group)], db.at[s, pl.ds(width, width)], down_sem.at[1, s]),
         )
 
     theirs = pl.ds(pl.multiple_of((1 - core) * half, half), half)
@@ -323,6 +317,13 @@
             pl.when(t == TILES - 1)(lambda: start_x(i // TILES + 2))
 
         events(i, 0)
+        pl.when(g == -1)(lambda: swap_down.wait())
+
+        @pl.when((g >= -1) & (g < n - 1))
+        def _():
+            for copy in load_down(g + 1):
+                copy.start()
+
         @pl.when((g >= 0) & (g < n))
         def _():
             for copy in load_down(g):
@@ -335,18 +336,11 @@
                         swap_hidden((g // TILES) * TILES + t, size).wait()
 
                 part[lax.rem(g, KEEP), 0:size] = jnp.dot(
-                    hidden[lax.rem(g // TILES, 2), 0:size], db[...], preferred_element_type=jnp.float32
+                    hidden[lax.rem(g // TILES, 2), 0:size], db[lax.rem(g, 2)], preferred_element_type=jnp.float32
                 )
                 sum1(g, size, row)
 
             by_size(g // TILES, dot)
-
-        pl.when(g == -1)(lambda: swap_down.wait())
-
-        @pl.when((g >= -1) & (g < n - 1))
-        def _():
-            for copy in load_down(g + 1):
-                copy.start()
 
         pl.when(i < n)(lambda: by_size(i // TILES, lambda size, row: swap_hidden(i, size).start()))
         events(i, 1)
@@ -372,7 +366,7 @@
             pltpu.VMEM((2, most, depth), b16),
             pltpu.VMEM((2, depth, tile), b16),
             pltpu.VMEM((2, depth, tile), b16),
-            pltpu.VMEM((2 * width, group), b16),
+            pltpu.VMEM((2, 2 * width, group), b16),
             pltpu.VMEM((2, most, 2 * width), b16),
             pltpu.VMEM((most, tile), f32),
             pltpu.VMEM((KEEP, most, group), f32),
@@ -385,7 +379,7 @@
             pltpu.VMEM((SLOTS, most // 2, group), b16),
             pltpu.VMEM((SLOTS, most // 4, group), b16),
             pltpu.VMEM((SLOTS, most // 8, group), b16),
-            dma((2, 2)), dma((2, SPLIT)), dma((2,)), dma((2,)), dma((2, TILES)), dma((2, TILES)), dma, dma, dma((len(PARTS), SLOTS)),
+            dma((2, 2)), dma((2, SPLIT)), dma((2,)), dma((2, 2)), dma((2, TILES)), dma((2, TILES)), dma, dma, dma((len(PARTS), SLOTS)),
             dma((6, len(PARTS), SLOTS)), dma((6, len(PARTS), SLOTS)), dma((len(SIZES) * TILES,)), dma((len(SIZES) * TILES,)),
         ],
         compiler_params=pltpu.CompilerParams(

time: 338 us -> 331 us (0.979)
  Pallas kernels: 315 us -> 308 us
    pallas_call x1, Pallas kernels: 315 us -> 308 us  [block(): pl.pallas_call(kernel, out_shape=(jax.ShapeDtypeStruct((rows, depth), b16...]
where the time goes in v3:
time: 331 us
  Pallas kernels  308 us (93%)
  local copies, waits for them, and re-layouts  23 us (7%)
    pallas_call x1, Pallas kernels, block(): pl.pallas_call(kernel, out_shape=(jax.ShapeDtypeStruct((rows, depth), b16...  308 us
    unnamed x1, local copies, waits for them, and re-layouts  23 us

profile of v3, /device:TPU:0, one launch (start us, length us, event | category | flops | bytes accessed | tf_op | source)
XLA Modules:
  0.0 330.7 jit_solution(11691457199181519030)
XLA Ops:
  0.0 307.7 %shard_map.46 = (bf16[2048,8192]{1,0:T(8,128)(2,1)}, bf16[2048,4096]{1,0:T(8,128)(2,1)}) custom-call(bf16[2048,8192]{1,0:T(8,128)(2,1)} %x_ref.1, bf16[8192,2048]{1,0:T(8,128)(2,1)} %gate_ref.1, bf16[8192,2048]{1,0:T(8,128)(2,1)} %up_ref.1, bf16[2048,8192]{1,0:T(8,128)(2,1)} %down_ref.1), custom_call_target="tpu_custom_call" | custom-call | flops 206158430208 | bytes 134217728 | tf_op jit(solution)/shard_map/pallas_call | solution.py:360
  307.7 23.0 %copy.6 = bf16[2048,8192]{1,0:T(8,128)(2,1)} copy(bf16[2048,8192]{1,0:T(8,128)(2,1)} %get-tuple-element.6) | data formatting | bytes 67108864
